TPU v7x, 32 devices: a whole 2x2x4 slice. The times are simulated.
32 devices in a mesh: dp: 8 (over z, core), seq: 4 (over y, x).
Axes of the slice: x: 2, y: 2, z: 4, core: 2. Of those that a mesh axis runs over, the one named last changes fastest.
Arguments:
- layer_in: bfloat16 [8, 512, 2560], P('dp', 'seq'), may hold values from -6 to 6
- scan_in: bfloat16 [8, 512, 2560], P('dp', 'seq'), may hold values from -6 to 6
- step_size: float32 [8, 512, 40], P('dp', 'seq'), may hold values from 0.0024 to 0.041
- b_weight: bfloat16 [2560, 64], replicated, may hold values from -0.125 to 0.125
- c_weight: bfloat16 [2560, 64], replicated, may hold values from -0.125 to 0.125
- decay_rate: float32 [40], replicated, may hold values from 0.0005 to 10
- skip_gain: float32 [40], replicated, may hold values from 0.25 to 1.75
- out_grad: bfloat16 [8, 512, 2560], P('dp', 'seq'), may hold values from -6 to 6
- doc_lengths: int32 [8, 4], P('dp'), may hold values from 1 to 256, 512 in all within a row
- block_order: int32 [8, 4], P('dp'), may hold values from 0 to 3, each once within a row
Outputs:
- scan_out: bfloat16 [8, 512, 2560], P('dp', 'seq')
- b_weight_grad: float32 [2560, 64], replicated
- c_weight_grad: float32 [2560, 64], replicated
Inputs may be any that keep to these rules, and one draw needn't show every extreme that they name: `block_order`: each row holds 0 to 3 once each. `doc_lengths`: each row sums to 512; its longest document has 256 tokens.
All inputs are finite; a program needn't handle non-finite values.
Results may differ from a plain program's by a relative error of at most 0.0055.
Values sent between devices are 32-bit elements.
A program may use at most 128 MiB of HBM per device.

v0:
```python
import math
import jax
import jax.numpy as jnp
from jax import lax
from jax.sharding import PartitionSpec as P

precise = lax.Precision.HIGHEST


def link_weights(low_block, high_block, totals):
    block_count = totals.shape[0]
    places = jnp.arange(block_count, dtype=jnp.int32)
    inside = (low_block[:, None] < places[None, :]) & (places[None, :] < high_block[:, None])
    factors = jnp.where(inside[:, :, None], totals[None, :, :], jnp.float32(1.0))
    return jnp.prod(factors, axis=1) * (low_block < high_block).astype(jnp.float32)[:, None]


def per_device(
    layer_in,
    scan_in,
    step_size,
    b_weight,
    c_weight,
    decay_rate,
    skip_gain,
    out_grad,
    doc_lengths,
    block_order,
):
    row_count = scan_in.shape[1]
    head_count = decay_rate.shape[0]
    head_width = scan_in.shape[2] // head_count
    state_count = b_weight.shape[1]
    block_count = lax.axis_size("seq")
    group_count = lax.axis_size("dp")
    my_slot = lax.axis_index("seq")
    tokens = layer_in[0]
    b_mat = jnp.dot(tokens, b_weight, preferred_element_type=jnp.float32).astype(jnp.bfloat16)
    c_mat = jnp.dot(tokens, c_weight, preferred_element_type=jnp.float32).astype(jnp.bfloat16)
    b_float = b_mat.astype(jnp.float32)
    c_float = c_mat.astype(jnp.float32)
    order_row = block_order[0]
    my_block = lax.dynamic_index_in_dim(order_row, my_slot, 0, keepdims=False)
    lengths = doc_lengths[0]
    doc_ends = jnp.cumsum(lengths, dtype=jnp.int32)
    doc_starts = doc_ends - lengths
    positions = my_block * row_count + jnp.arange(row_count, dtype=jnp.int32)
    segment = jnp.sum((doc_starts[None, :] <= positions[:, None]).astype(jnp.int32), axis=1)
    begins = jnp.any(doc_starts[None, :] == positions[:, None], axis=1)
    step_sizes = step_size[0]
    log_rates = -step_sizes * decay_rate[None, :]
    offsets = jnp.arange(row_count, dtype=jnp.int32)
    lower_tri = offsets[:, None] >= offsets[None, :]
    cumlog = jnp.dot(lower_tri.astype(jnp.float32), log_rates, precision=precise)
    linked = (segment == segment[0]) & jnp.logical_not(begins[0])
    in_last = segment == segment[row_count - 1]
    entering = jnp.where(linked[:, None], jnp.exp(cumlog), jnp.float32(0.0))
    leaving = jnp.where(
        in_last[:, None], jnp.exp(cumlog[row_count - 1][None, :] - cumlog), jnp.float32(0.0)
    )
    block_total = entering[row_count - 1]
    x_heads = scan_in[0].reshape(row_count, head_count, head_width)
    grad_heads = out_grad[0].reshape(row_count, head_count, head_width)
    driven = x_heads.astype(jnp.float32) * step_sizes[:, :, None]
    pushed = driven * leaving[:, :, None]
    seen = grad_heads.astype(jnp.float32) * entering[:, :, None]
    own_state = jnp.einsum("thp,tn->hpn", pushed, b_float, precision=precise).reshape(
        head_count, head_width * state_count
    )
    own_adjoint = jnp.einsum("thp,tn->hpn", seen, c_float, precision=precise).reshape(
        head_count, head_width * state_count
    )
    all_totals = lax.all_gather(block_total[None, :], "seq", axis=0, tiled=True)
    held_slots = jnp.arange(block_count, dtype=jnp.int32)
    onehot = (order_row[None, :] == held_slots[:, None]).astype(jnp.float32)
    seq_totals = jnp.dot(onehot, all_totals, precision=precise)
    mine_vector = jnp.full((block_count,), my_block, jnp.int32)
    from_earlier = link_weights(order_row, mine_vector, seq_totals)
    from_later = link_weights(mine_vector, order_row, seq_totals)
    incoming = jnp.einsum(
        "ch,chz->hz",
        from_earlier,
        lax.all_gather(own_state[None], "seq", axis=0, tiled=True),
        precision=precise,
    )
    returning = jnp.einsum(
        "ch,chz->hz",
        from_later,
        lax.all_gather(own_adjoint[None], "seq", axis=0, tiled=True),
        precision=precise,
    )
    incoming = incoming.reshape(head_count, head_width, state_count)
    returning = returning.reshape(head_count, head_width, state_count)
    scores = jnp.einsum("tn,sn->ts", c_mat, b_mat, preferred_element_type=jnp.float32)
    causal = lower_tri & (segment[:, None] == segment[None, :])
    set_size = math.gcd(head_count, 16)
    set_count = head_count // set_size

    def per_set(set_index, totals_pair):
        out_acc, mix_acc = totals_pair
        head_first = set_index * set_size
        set_log = lax.dynamic_slice_in_dim(cumlog, head_first, set_size, 1)
        set_steps = lax.dynamic_slice_in_dim(step_sizes, head_first, set_size, 1)
        set_driven = lax.dynamic_slice_in_dim(driven, head_first, set_size, 1)
        set_inputs = lax.dynamic_slice_in_dim(x_heads, head_first, set_size, 1)
        set_cotan = lax.dynamic_slice_in_dim(grad_heads, head_first, set_size, 1)
        log_gaps = set_log.T[:, :, None] - set_log.T[:, None, :]
        decays = jnp.exp(jnp.where(causal[None], log_gaps, jnp.float32(-1e30)))
        mixed = decays * scores[None]
        y_part = jnp.einsum("hts,shp->thp", mixed, set_driven, precision=precise)
        intersect = jnp.einsum(
            "thp,shp->hts", set_cotan, set_inputs, preferred_element_type=jnp.float32
        )
        q_part = jnp.sum(decays * intersect * set_steps.T[:, None, :], axis=0)
        out_acc = lax.dynamic_update_slice_in_dim(out_acc, y_part, head_first, 1)
        return (out_acc, mix_acc + q_part)

    start_pair = (
        jnp.zeros((row_count, head_count, head_width), jnp.float32),
        jnp.zeros((row_count, row_count), jnp.float32),
    )
    y_intra, mixing = lax.fori_loop(0, set_count, per_set, start_pair)
    y_cross = jnp.einsum("tn,hpn->thp", c_float, incoming, precision=precise) * entering[:, :, None]
    y_total = y_intra + y_cross + skip_gain[None, :, None] * x_heads.astype(jnp.float32)
    scan_out = y_total.reshape(row_count, head_count * head_width).astype(jnp.bfloat16)[None]
    grad_c = jnp.dot(mixing, b_float, precision=precise) + jnp.einsum(
        "thp,hpn->tn", seen, incoming, precision=precise
    )
    grad_b = jnp.einsum("ts,tn->sn", mixing, c_float, precision=precise) + jnp.einsum(
        "thp,hpn->tn", pushed, returning, precision=precise
    )
    local_b = jnp.einsum(
        "td,tn->dn", tokens, grad_b.astype(jnp.bfloat16), preferred_element_type=jnp.float32
    )
    local_c = jnp.einsum(
        "td,tn->dn", tokens, grad_c.astype(jnp.bfloat16), preferred_element_type=jnp.float32
    )
    summed_b, summed_c = lax.psum((local_b, local_c), ("dp", "seq"))
    scale = 1.0 / (group_count * row_count * block_count)
    return (scan_out, summed_b * scale, summed_c * scale)


def solution(mesh):
    in_specs = (
        P("dp", "seq", None),
        P("dp", "seq", None),
        P("dp", "seq", None),
        P(),
        P(),
        P(),
        P(),
        P("dp", "seq", None),
        P("dp", None),
        P("dp", None),
    )
    out_specs = (P("dp", "seq", None), P(), P())
    return jax.shard_map(
        per_device, mesh=mesh, in_specs=in_specs, out_specs=out_specs, check_vma=False
    )
```

profile of v0, /device:TPU:0, one launch (start us, length us, event | category | flops | bytes accessed | tf_op | source)
XLA Modules:
  0.0 262.6 jit_solution(5989525888902868005)
XLA Ops:
  7.3 1.3 constant_dynamic-slice_fusion
  9.2 0.8 reduce-window_clone.1
  10.9 1.4 copy.37
  13.7 1.3 broadcast_compare_fusion
  16.0 1.3 broadcast_in_dim_reshape.6
  19.3 1.3 broadcast_in_dim_reshape.7
  20.7 1.3 convert_multiply_fusion.1
  24.2 1.2 bitcast_multiply_fusion.1
  25.4 1.2 bitcast_multiply_fusion
  26.6 9.7 %all-gather = f32[4,1,40]{2,1,0:T(1,128)S(1)} all-gather(f32[1,1,40]{2,1,0:T(1,128)S(1)} %bitcast.112), channel_id=1, replica_groups=mesh['dp'=8,'seq'=4] {'seq'}, dimensions={0}, use_global_device_ids=true | all-gather | bytes 800 | tf_op jit(solution)/shard_map/all_gather | solution.py:73
  37.1 13.5 %while.16 = (s32[]{:T(128)}, f32[128,40,64]{0,2,1:T(8,128)S(1)}, f32[128,128]{1,0:T(8,128)S(1)}, f32[128,40,64]{0,2,1:T(8,128)}, f32[128,40]{0,1:T(8,128)S(1)}, ...) while((s32[]{:T(128)}, f32[128,40,64]{0,2,1:T(8,128)S(1)}, ...), condition=%wide.region_4.5_spmd.clone, body=%wide.region_2.4_spmd.clone.sunk | while | flops 118554632 | bytes 1202889 | solution.py:122
  37.2 2.1 fusion.82
  39.9 2.1 fusion.82
  42.5 2.2 fusion.82
  45.2 2.1 fusion.82
  47.9 2.1 fusion.82
  50.6 9.0 %all-gather.4.cloned.1.call-done = f32[4,40,4096]{2,1,0:T(8,128)} async-done(((f32[1,40,4096]{2,1,0:T(8,128)}), f32[4,40,4096]{2,1,0:T(8,128)}) %all-gather.4.cloned.1.call-update) | async-done | bytes 2621456 | tf_op jit(solution)/shard_map/all_gather | solution.py:83
  59.7 8.0 %fusion.20 = f32[40,1,4096]{2,1,0:T(1,128)S(1)} fusion(f32[4,40,1]{0,2,1:T(1,128)S(1)} %copy.44, f32[4,40,4096]{2,1,0:T(8,128)} %all-gather.4.cloned.1.call-done), kind=kOutput, calls=%fused_computation.28 | convolution fusion | flops 7864320 | bytes 3277440 | tf_op jit(solution)/shard_map/ch,chz->hz/dot_general | solution.py:80
  67.6 1.2 copy.59
  68.9 1.7 reshape.147
  70.5 31.1 %all-gather.6.cloned.1.call-done = f32[4,40,4096]{2,1,0:T(8,128)} async-done(((f32[1,40,4096]{2,1,0:T(8,128)}), f32[4,40,4096]{2,1,0:T(8,128)}) %all-gather.6.cloned.1.call-update) | async-done | bytes 2621456 | tf_op jit(solution)/shard_map/all_gather | solution.py:89
  101.6 8.2 %fusion.18 = f32[40,1,4096]{2,1,0:T(1,128)S(1)} fusion(f32[4,40,1]{0,2,1:T(1,128)S(1)} %copy.47, f32[4,40,4096]{2,1,0:T(8,128)} %all-gather.6.cloned.1.call-done), kind=kOutput, calls=%fused_computation.26 | convolution fusion | flops 7864320 | bytes 3277440 | tf_op jit(solution)/shard_map/ch,chz->hz/dot_general | solution.py:86
  110.2 1.6 reshape.148
  111.8 4.0 %convolution_bitcast_fusion.4 = f32[128,64]{0,1:T(8,128)S(1)} fusion(f32[128,40,64]{0,2,1:T(8,128)} %bitcast.101, f32[40,64,64]{2,1,0:T(8,128)} %reshape.148), kind=kOutput, calls=%fused_computation.47 | convolution fusion | flops 251658240 | bytes 1998848 | tf_op jit(solution)/shard_map/thp,hpn->tn/dot_general | solution.py:129
  116.0 1.1 convolution_bitcast_fusion.2
  117.1 2.3 convolution_bitcast_fusion.3
  119.7 1.1 convolution_bitcast_fusion.1
  120.8 2.2 fusion.24
  123.0 1.1 copy.43
  124.1 129.1 %all-reduce.3.cloned.1.call-done = (f32[2560,64]{0,1:T(8,128)}, f32[2560,64]{0,1:T(8,128)}) async-done(((f32[2560,64]{0,1:T(8,128)}, f32[2560,64]{0,1:T(8,128)}), (f32[2560,64]{0,1:T(8,128)}, f32[2560,64]{0,1:T(8,128)})) %all-reduce.3.cloned.1.call-update) | async-done | bytes 1310736 | tf_op jit(solution)/shard_map/psum | solution.py:138
  253.1 2.0 broadcast_multiply_fusion.1
  255.2 0.9 broadcast_multiply_fusion
  (77 shorter events, 11.3 us)
Async XLA Ops:
  7.2 6.2 %copy-start = (bf16[1,128,2560]{2,1,0:T(8,128)(2,1)S(1)}, bf16[1,128,2560]{2,1,0:T(8,128)(2,1)}, u32[]{:S(2)}) copy-start(bf16[1,128,2560]{2,1,0:T(8,128)(2,1)} %param.12) | copy-start | bytes 1966084
  7.2 5.1 %copy-start.5 = (f32[1,128,40]{1,2,0:T(8,128)S(1)}, f32[1,128,40]{1,2,0:T(8,128)}, u32[]{:S(2)}) copy-start(f32[1,128,40]{1,2,0:T(8,128)} %param.14) | copy-start | bytes 61444
  7.2 5.1 %copy-start.10 = (f32[40]{0:T(128)S(1)}, f32[40]{0:T(128)}, u32[]{:S(2)}) copy-start(f32[40]{0:T(128)} %param.17) | copy-start | bytes 484
  7.2 6.2 %copy-start.6 = (bf16[2560,64]{0,1:T(8,128)(2,1)S(1)}, bf16[2560,64]{0,1:T(8,128)(2,1)}, u32[]{:S(2)}) copy-start(bf16[2560,64]{0,1:T(8,128)(2,1)} %param.15) | copy-start | bytes 983044
  7.2 52.4 %all-gather.4.cloned.1.call-start = ((), (), s32[]{:S(2)}) async-start(), calls=%async_computation | async-start | bytes 3276800 | tf_op jit(solution)/shard_map/all_gather | solution.py:83
  15.9 1.4 copy-start.3
  17.2 1.0 copy-start.7
  17.3 84.4 %all-gather.6.cloned.1.call-start = ((), (), s32[]{:S(2)}) async-start(), calls=%async_computation.1 | async-start | bytes 3276800 | tf_op jit(solution)/shard_map/all_gather | solution.py:89
  20.6 3.0 %copy-start.8 = (s32[1,4]{1,0:T(1,128)S(1)}, s32[1,4]{1,0:T(1,128)}, u32[]{:S(2)}) copy-start(s32[1,4]{1,0:T(1,128)} %param.21) | copy-start | bytes 52
  20.6 232.5 %all-reduce.3.cloned.1.call-start = ((), (), s32[]{:S(2)}) async-start(), calls=%async_computation.2 | async-start | bytes 2621440 | tf_op jit(solution)/shard_map/psum | solution.py:138
  50.6 17.0 %copy-start.1 = (f32[128,40,64]{0,2,1:T(8,128)}, f32[128,40,64]{0,2,1:T(8,128)S(1)}, u32[]{:S(2)}) copy-start(f32[128,40,64]{0,2,1:T(8,128)S(1)} %get-tuple-element.173) | copy-start | bytes 3932164
  115.8 1.3 copy-start.2
  119.7 1.1 copy-start.9
  253.1 2.0 copy-start.4
Sparse Core Ops, SparseCore 0:
  17.4 42.2 all-gather.3
  62.1 39.5 all-gather.5
  120.9 132.1 all-reduce.2
where the time goes:
time: 263 us
  waiting for transfers between devices  169 us (64%)
  matrix products  43.1 us (16%)
  between operations  14.7 us (6%)
  local copies, waits for them, and re-layouts  13.5 us (5%)
  other arithmetic  11.7 us (4%)
  blocking collectives  9.7 us (4%)
    psum x1, waiting for transfers between devices, per_device(): summed_b, summed_c = lax.psum((local_b, local_c), ('dp', 'seq'))  129 us
    all_gather x1, waiting for transfers between devices, per_device(): lax.all_gather(own_adjoint[None], 'seq', axis=0, tiled=True)  31.1 us
    dot_general x5, matrix products, per_set(): y_part = jnp.einsum('hts,shp->thp', mixed, set_driven, precision=precise)  10.7 us
    all_gather x1, blocking collectives, per_device(): all_totals = lax.all_gather(block_total[None, :], 'seq', axis=0, tiled=True)  9.7 us
    all_gather x1, waiting for transfers between devices, per_device(): lax.all_gather(own_state[None], 'seq', axis=0, tiled=True)  9.04 us
    dot_general x1, matrix products, per_device(): jnp.einsum('ch,chz->hz', from_later, lax.all_gather(own_adjoint[None], 's...  8.21 us
    dot_general x1, matrix products, per_device(): jnp.einsum('ch,chz->hz', from_earlier, lax.all_gather(own_state[None], 's...  7.98 us
  transfers between devices with their start and end apart: 3, of which 3 were waited for; matrix products, arithmetic and copies ran while one was open for 14% of the time, Pallas kernels for 0%

commit v1 on v0

--- a/solution.py
+++ b/solution.py
@@ -83,12 +83,26 @@
         lax.all_gather(own_state[None], "seq", axis=0, tiled=True),
         precision=precise,
     )
+    size, here = (lax.axis_size("seq"), lax.axis_index("seq"))
+    left = [(i, (i - 1) % size) for i in range(size)]
+    rows = own_adjoint[None].shape[0]
+    held = own_adjoint[None]
     returning = jnp.einsum(
         "ch,chz->hz",
-        from_later,
-        lax.all_gather(own_adjoint[None], "seq", axis=0, tiled=True),
+        lax.dynamic_slice_in_dim(from_later, here * rows, held.shape[0], axis=0),
+        held,
         precision=precise,
     )
+    for step in range(1, size):
+        held = lax.ppermute(held, "seq", left)
+        returning = returning + jnp.einsum(
+            "ch,chz->hz",
+            lax.dynamic_slice_in_dim(
+                from_later, (here + step) % size * rows, held.shape[0], axis=0
+            ),
+            held,
+            precision=precise,
+        )
     incoming = incoming.reshape(head_count, head_width, state_count)
     returning = returning.reshape(head_count, head_width, state_count)
     scores = jnp.einsum("tn,sn->ts", c_mat, b_mat, preferred_element_type=jnp.float32)

time: 263 us -> 266 us (1.011)
  starting transfers between devices: 0.12 us -> 6.82 us
  waiting for transfers between devices: 169 us -> 164 us
  local copies, waits for them, and re-layouts: 13.5 us -> 17.1 us
    ppermute x0 -> x3, waiting for transfers between devices: none -> 34.3 us  [per_device(): held = lax.ppermute(held, 'seq', left)]
    all_gather x1 -> x0, waiting for transfers between devices: 31.1 us -> none  [per_device(): lax.all_gather(own_adjoint[None], 'seq', axis=0, tiled=True)]
    all_gather x1, waiting for transfers between devices: 9.04 us -> 0.01 us  [per_device(): lax.all_gather(own_state[None], 'seq', axis=0, tiled=True)]
    dot_general x1 -> x0, matrix products: 8.21 us -> none  [per_device(): jnp.einsum('ch,chz->hz', from_later, lax.all_gather(own_adjoint[None], 's...]
    ppermute x0 -> x3, starting transfers between devices: none -> 6.74 us  [per_device(): held = lax.ppermute(held, 'seq', left)]
    dot_general x5, matrix products: 10.7 us -> 14.2 us  [per_set(): y_part = jnp.einsum('hts,shp->thp', mixed, set_driven, precision=precise)]
  transfers between devices with their start and end apart: 3 -> 5, of which waited for: 3 -> 3; matrix products, arithmetic and copies ran while one was open for 14% -> 16% of each run, Pallas kernels for 0% -> 0%
where the time goes in v1:
time: 266 us; the launch traced here: 265 us
  waiting for transfers between devices  164 us (62%)
  matrix products  42 us (16%)
  local copies, waits for them, and re-layouts  17.1 us (6%)
  between operations  14.9 us (6%)
  other arithmetic  12.4 us (5%)
  blocking collectives  7.22 us (3%)
  starting transfers between devices  6.82 us (3%)
    psum x1, waiting for transfers between devices, per_device(): summed_b, summed_c = lax.psum((local_b, local_c), ('dp', 'seq'))  130 us
    ppermute x3, waiting for transfers between devices, per_device(): held = lax.ppermute(held, 'seq', left)  34.3 us
    dot_general x5, matrix products, per_set(): y_part = jnp.einsum('hts,shp->thp', mixed, set_driven, precision=precise)  14.2 us
    dot_general x1, matrix products, per_device(): jnp.einsum('ch,chz->hz', from_earlier, lax.all_gather(own_state[None], 's...  7.97 us
    all_gather x1, blocking collectives, per_device(): all_totals = lax.all_gather(block_total[None, :], 'seq', axis=0, tiled=True)  7.22 us
    ppermute x3, starting transfers between devices, per_device(): held = lax.ppermute(held, 'seq', left)  6.74 us
  transfers between devices with their start and end apart: 5, of which 3 were waited for; matrix products, arithmetic and copies ran while one was open for 16% of the time, Pallas kernels for 0%

profile of v1, /device:TPU:0, one launch (start us, length us, event | category | flops | bytes accessed | tf_op | source)
XLA Modules:
  0.0 265.1 jit_solution(14909201139839535621)
XLA Ops:
  7.2 1.3 constant_dynamic-slice_fusion.4
  12.6 1.4 copy.38
  14.4 1.3 broadcast_compare_fusion
  16.6 1.3 broadcast_in_dim_reshape.7
  17.8 3.9 %collective-permute-start = (f32[1,40,4096]{2,1,0:T(8,128)}, f32[1,40,4096]{2,1,0:T(8,128)}, u32[]{:S(2)}, u32[]{:S(2)}) collective-permute-start(f32[1,40,4096]{2,1,0:T(8,128)} %broadcast_in_dim_reshape.7), channel_id=1, source_target_pairs={{0,3},{1,0},{2,1},{3,2},{4,7},{5,4},{6,5},{7,6},{8,11},{9,8},{10,9... | collective-permute-start | bytes 1966088 | tf_op jit(solution)/shard_map/ppermute | solution.py:97
  21.7 1.4 copy.37
  23.2 1.3 convolution_convert_fusion
  24.5 1.9 fusion.26
  26.4 2.6 broadcast_in_dim_reshape.6
  29.0 1.3 convert_multiply_fusion.1
  31.1 1.2 broadcast_in_dim.120
  32.4 16.7 %while.16 = (s32[]{:T(128)}, f32[128,40,64]{0,2,1:T(8,128)}, f32[128,128]{1,0:T(8,128)S(1)}, f32[128,40,64]{0,2,1:T(8,128)}, f32[128,40]{0,1:T(8,128)S(1)}, /*in...) while((s32[]{:T(128)}, f32[128,40,64]{0,2,1:T(8,128)}, ...), condition=%wide.region_4.5_spmd.clone, body=%wide.region_2.4_spmd.clone.sunk | while | flops 118554632 | bytes 1202881 | solution.py:136
  32.4 2.8 %fusion.86 = f32[128,40,64]{0,2,1:T(8,128)} fusion(f32[128,40,64]{0,2,1:T(8,128)} %get-tuple-element.347, s32[]{:T(128)S(6)} %select_n.91, f32[128,128]{1,0:T(8,128)} %get-tuple-element.365, f32[8,128]{1,0:T(8,128)S(1)} %get-tuple-element.330, f32[128,40,64]{0,2,1:T(8,128)} %get-tuple-element.363, pred[128,128]{1,0:T(8,128)(4,1)S(1)} %fusion.85), kind=kOutput, calls=%fused_computation.5.clone.1 | convolution fusion | flops 101056512 | bytes 615424 | tf_op jit(solution)/shard_map/while/body/eval_jaxpr/hts,shp->thp/dot_general | solution.py:124
  35.8 2.8 %fusion.86 = f32[128,40,64]{0,2,1:T(8,128)} fusion(f32[128,40,64]{0,2,1:T(8,128)} %get-tuple-element.347, s32[]{:T(128)S(6)} %select_n.91, f32[128,128]{1,0:T(8,128)} %get-tuple-element.365, f32[8,128]{1,0:T(8,128)S(1)} %get-tuple-element.330, f32[128,40,64]{0,2,1:T(8,128)} %get-tuple-element.363, pred[128,128]{1,0:T(8,128)(4,1)S(1)} %fusion.85), kind=kOutput, calls=%fused_computation.5.clone.1 | convolution fusion | flops 101056512 | bytes 615424 | tf_op jit(solution)/shard_map/while/body/eval_jaxpr/hts,shp->thp/dot_general | solution.py:124
  39.1 2.8 %fusion.86 = f32[128,40,64]{0,2,1:T(8,128)} fusion(f32[128,40,64]{0,2,1:T(8,128)} %get-tuple-element.347, s32[]{:T(128)S(6)} %select_n.91, f32[128,128]{1,0:T(8,128)} %get-tuple-element.365, f32[8,128]{1,0:T(8,128)S(1)} %get-tuple-element.330, f32[128,40,64]{0,2,1:T(8,128)} %get-tuple-element.363, pred[128,128]{1,0:T(8,128)(4,1)S(1)} %fusion.85), kind=kOutput, calls=%fused_computation.5.clone.1 | convolution fusion | flops 101056512 | bytes 615424 | tf_op jit(solution)/shard_map/while/body/eval_jaxpr/hts,shp->thp/dot_general | solution.py:124
  42.5 2.8 %fusion.86 = f32[128,40,64]{0,2,1:T(8,128)} fusion(f32[128,40,64]{0,2,1:T(8,128)} %get-tuple-element.347, s32[]{:T(128)S(6)} %select_n.91, f32[128,128]{1,0:T(8,128)} %get-tuple-element.365, f32[8,128]{1,0:T(8,128)S(1)} %get-tuple-element.330, f32[128,40,64]{0,2,1:T(8,128)} %get-tuple-element.363, pred[128,128]{1,0:T(8,128)(4,1)S(1)} %fusion.85), kind=kOutput, calls=%fused_computation.5.clone.1 | convolution fusion | flops 101056512 | bytes 615424 | tf_op jit(solution)/shard_map/while/body/eval_jaxpr/hts,shp->thp/dot_general | solution.py:124
  45.8 2.8 %fusion.86 = f32[128,40,64]{0,2,1:T(8,128)} fusion(f32[128,40,64]{0,2,1:T(8,128)} %get-tuple-element.347, s32[]{:T(128)S(6)} %select_n.91, f32[128,128]{1,0:T(8,128)} %get-tuple-element.365, f32[8,128]{1,0:T(8,128)S(1)} %get-tuple-element.330, f32[128,40,64]{0,2,1:T(8,128)} %get-tuple-element.363, pred[128,128]{1,0:T(8,128)(4,1)S(1)} %fusion.85), kind=kOutput, calls=%fused_computation.5.clone.1 | convolution fusion | flops 101056512 | bytes 615424 | tf_op jit(solution)/shard_map/while/body/eval_jaxpr/hts,shp->thp/dot_general | solution.py:124
  49.0 1.3 reshape.174
  51.8 7.2 %all-gather = f32[4,1,40]{2,1,0:T(1,128)S(1)} all-gather(f32[1,1,40]{2,1,0:T(1,128)S(1)} %bitcast.130), channel_id=1, replica_groups=mesh['dp'=8,'seq'=4] {'seq'}, dimensions={0}, use_global_device_ids=true | all-gather | bytes 800 | tf_op jit(solution)/shard_map/all_gather | solution.py:73
  59.6 1.5 collective-permute-start.1
  61.9 20.0 %collective-permute-done.1 = f32[1,40,4096]{2,1,0:T(8,128)S(1)} collective-permute-done((f32[1,40,4096]{2,1,0:T(8,128)}, f32[1,40,4096]{2,1,0:T(8,128)S(1)}, u32[]{:S(2)}, u32[]{:S(2)}) %collective-permute-start.1) | collective-permute-done | bytes 655392 | tf_op jit(solution)/shard_map/ppermute | solution.py:97
  81.9 1.3 collective-permute-start.2
  83.6 14.3 %collective-permute-done.2 = f32[1,40,4096]{2,1,0:T(8,128)} collective-permute-done((f32[1,40,4096]{2,1,0:T(8,128)S(1)}, f32[1,40,4096]{2,1,0:T(8,128)}, u32[]{:S(2)}, u32[]{:S(2)}) %collective-permute-start.2) | collective-permute-done | bytes 655392 | tf_op jit(solution)/shard_map/ppermute | solution.py:97
  97.9 1.9 fusion.30
  99.8 1.6 reshape.181
  101.4 3.6 %convolution_bitcast_fusion.4 = f32[128,64]{0,1:T(8,128)S(1)} fusion(f32[128,40,64]{0,2,1:T(8,128)S(1)} %bitcast.121, f32[40,64,64]{2,1,0:T(8,128)} %reshape.181), kind=kOutput, calls=%fused_computation.45 | convolution fusion | flops 251658240 | bytes 1998848 | tf_op jit(solution)/shard_map/thp,hpn->tn/dot_general | solution.py:143
  106.3 8.0 %fusion.18 = f32[40,1,4096]{2,1,0:T(1,128)S(1)} fusion(f32[4,40,1]{0,2,1:T(1,128)S(1)} %copy.44, f32[4,40,4096]{2,1,0:T(8,128)} %all-gather.3.cloned.1.call-done), kind=kOutput, calls=%fused_computation.26 | convolution fusion | flops 7864320 | bytes 3277440 | tf_op jit(solution)/shard_map/ch,chz->hz/dot_general | solution.py:80
  115.5 1.6 reshape.172
  117.1 3.6 %convolution_bitcast_fusion.3 = f32[128,64]{0,1:T(8,128)S(1)} fusion(f32[128,40,64]{0,2,1:T(8,128)} %bitcast.120, f32[40,64,64]{2,1,0:T(8,128)S(1)} %reshape.172), kind=kOutput, calls=%fused_computation.44 | convolution fusion | flops 251658240 | bytes 1998848 | tf_op jit(solution)/shard_map/thp,hpn->tn/dot_general | solution.py:140
  122.1 2.2 fusion.22
  125.3 130.0 %all-reduce.3.cloned.1.call-done = (f32[2560,64]{0,1:T(8,128)}, f32[2560,64]{0,1:T(8,128)}) async-done(((f32[2560,64]{0,1:T(8,128)}, f32[2560,64]{0,1:T(8,128)}), (f32[2560,64]{0,1:T(8,128)}, f32[2560,64]{0,1:T(8,128)})) %all-reduce.3.cloned.1.call-update) | async-done | bytes 1310736 | tf_op jit(solution)/shard_map/psum | solution.py:152
  255.3 2.0 broadcast_multiply_fusion
  (72 shorter events, 16.6 us)
Async XLA Ops:
  7.2 6.9 %copy-start = (bf16[1,128,2560]{2,1,0:T(8,128)(2,1)S(1)}, bf16[1,128,2560]{2,1,0:T(8,128)(2,1)}, u32[]{:S(2)}) copy-start(bf16[1,128,2560]{2,1,0:T(8,128)(2,1)} %param.12) | copy-start | bytes 1966084
  7.2 6.9 %copy-start.4 = (bf16[2560,64]{0,1:T(8,128)(2,1)S(1)}, bf16[2560,64]{0,1:T(8,128)(2,1)}, u32[]{:S(2)}) copy-start(bf16[2560,64]{0,1:T(8,128)(2,1)} %param.16) | copy-start | bytes 983044
  7.2 99.1 %all-gather.3.cloned.1.call-start = ((), (), s32[]{:S(2)}) async-start(), calls=%async_computation | async-start | bytes 3276800 | tf_op jit(solution)/shard_map/all_gather | solution.py:83
  17.8 6.7 %copy-start.3 = (f32[1,128,40]{1,2,0:T(8,128)S(1)}, f32[1,128,40]{1,2,0:T(8,128)}, u32[]{:S(2)}) copy-start(f32[1,128,40]{1,2,0:T(8,128)} %param.14) | copy-start | bytes 61444
  17.8 41.8 %collective-permute-start = (f32[1,40,4096]{2,1,0:T(8,128)}, f32[1,40,4096]{2,1,0:T(8,128)}, u32[]{:S(2)}, u32[]{:S(2)}) collective-permute-start(f32[1,40,4096]{2,1,0:T(8,128)} %broadcast_in_dim_reshape.7), channel_id=1, source_target_pairs={{0,3},{1,0},{2,1},{3,2},{4,7},{5,4},{6,5},{7,6},{8,11},{9,8},{10,9... | collective-permute-start | bytes 1966088 | tf_op jit(solution)/shard_map/ppermute | solution.py:97
  29.0 226.4 %all-reduce.3.cloned.1.call-start = ((), (), s32[]{:S(2)}) async-start(), calls=%async_computation.1 | async-start | bytes 2621440 | tf_op jit(solution)/shard_map/psum | solution.py:152
  50.4 10.7 %copy-start.5 = (s32[1,4]{1,0:T(1,128)S(1)}, s32[1,4]{1,0:T(1,128)}, u32[]{:S(2)}) copy-start(s32[1,4]{1,0:T(1,128)} %param.21) | copy-start | bytes 52
  59.6 22.3 %collective-permute-start.1 = (f32[1,40,4096]{2,1,0:T(8,128)}, f32[1,40,4096]{2,1,0:T(8,128)S(1)}, u32[]{:S(2)}, u32[]{:S(2)}) collective-permute-start(f32[1,40,4096]{2,1,0:T(8,128)} %collective-permute-done), channel_id=1, source_target_pairs={{0,3},{1,0},{2,1},{3,2},{4,7},{5,4},{6,5},{7,6},{8,11},{9,8},{10,9... | collective-permute-start | bytes 1966088 | tf_op jit(solution)/shard_map/ppermute | solution.py:97
  81.9 16.0 %copy-start.2 = (f32[1,40,4096]{2,1,0:T(8,128)}, f32[1,40,4096]{2,1,0:T(8,128)S(1)}, u32[]{:S(2)}) copy-start(f32[1,40,4096]{2,1,0:T(8,128)S(1)} %collective-permute-done.1) | copy-start | bytes 1966084
  81.9 16.0 %collective-permute-start.2 = (f32[1,40,4096]{2,1,0:T(8,128)S(1)}, f32[1,40,4096]{2,1,0:T(8,128)}, u32[]{:S(2)}, u32[]{:S(2)}) collective-permute-start(f32[1,40,4096]{2,1,0:T(8,128)S(1)} %collective-permute-done.1), channel_id=1, source_target_pairs={{0,3},{1,0},{2,1},{3,2},{4,7},{5,4},{6,5},{7,6},{8,11},{9,8},{10,9... | collective-permute-start | bytes 1966088 | tf_op jit(solution)/shard_map/ppermute | solution.py:97
  120.9 1.1 copy-start.6
  255.3 2.0 copy-start.1
Sparse Core Ops, SparseCore 0:
  29.1 45.4 all-gather.2
  122.2 133.1 all-reduce.2
